TPU v7x, 32 devices: a whole 2x2x4 slice. The times are simulated.
32 devices in a mesh: lang: 2 (over y), clu: 16 (over z, x, core).
Axes of the slice: x: 2, y: 2, z: 4, core: 2. Of those that a mesh axis runs over, the one named last changes fastest.
Arguments:
- embeddings: bfloat16 [8192, 1024], P(('lang', 'clu')), parts along dimension 0, may hold values from -6 to 6
- assignment: int32 [8192, 1], P(('lang', 'clu')), parts along dimension 0, may hold values from 0 to 31; in each aligned block of 256 rows (0 to 255, 256 to 511, ...) at most 16 rows name the same one
Outputs:
- best_similarity: float32 [8192], P(('lang', 'clu')), parts along dimension 0
There are 2 independent parts, one for each index of `lang`. A program takes and returns all parts, laid end to end along the dimension named above; each array names one. Nothing has to cross between parts.
Inputs may be any that keep to these rules, and one draw needn't show every extreme that they name: `assignment`: in each aligned block of 256 rows (the rows of one device) no cluster is named by more than 16 rows; every cluster is named by some row.
All inputs are finite; a program needn't handle non-finite values.
Results may differ from a plain program's by a relative error of at most 0.0016.
Values may be sent and summed in bfloat16 or wider, within the bound.
A program may use at most 64 MiB of HBM per device.

v0:
```python
import jax
import jax.numpy as jnp
from jax import lax
from jax.sharding import PartitionSpec as P

CLU_DEV = 2


EPS = 1e-06


def normalize(embeddings):
    values = embeddings.astype(jnp.float32)
    scale = lax.rsqrt(jnp.sum(values * values, axis=-1, keepdims=True) + EPS)
    return (values * scale).astype(jnp.bfloat16)


def slot_index(cluster, groups, most):
    count = cluster.shape[0]
    order = jnp.argsort(cluster, stable=True)
    ranked = cluster[order]
    first = jnp.searchsorted(ranked, ranked, side="left")
    rank_sorted = jnp.arange(count, dtype=jnp.int32) - first
    rank = jnp.zeros((count,), jnp.int32).at[order].set(rank_sorted)
    local = cluster % CLU_DEV
    owner = cluster // CLU_DEV
    return (local * groups + owner) * most + rank


def cluster_scores(pieces):
    rows, flags = pieces
    items = rows.shape[0]
    width = rows.shape[1] * rows.shape[2]
    rows = rows.reshape(items, width, rows.shape[3])
    flags = flags.reshape(items, width)
    offsets = jnp.arange(width, dtype=jnp.int32)
    distinct = offsets[:, None] != offsets[None, :]

    def single(pair):
        block, marks = pair
        gram = lax.dot_general(
            block, block, (((1,), (1,)), ((), ())), preferred_element_type=jnp.float32
        )
        keep = distinct & (marks > 0)[None, :]
        best = jnp.max(jnp.where(keep, gram, jnp.float32(-2.0)), axis=1)
        return jnp.maximum(best, jnp.float32(-1.0))

    best = lax.map(single, (rows, flags))
    return best.reshape(items, 1, width)


def shards(embeddings, assignment):
    groups = lax.axis_size("clu")
    count = embeddings.shape[0]
    width = embeddings.shape[1]
    most = 2 * count // (CLU_DEV * groups)
    unit = normalize(embeddings)
    cluster = assignment[:, 0]
    slot = slot_index(cluster, groups, most)
    total = CLU_DEV * groups * most
    outgoing = jnp.zeros((total, width), jnp.bfloat16).at[slot].set(unit)
    marks = jnp.zeros((total,), jnp.bfloat16).at[slot].set(jnp.ones((count,), jnp.bfloat16))
    outgoing = outgoing.reshape(CLU_DEV, groups, most, width)
    marks = marks.reshape(CLU_DEV, groups, most)
    arrived = (
        lax.all_to_all(outgoing, "clu", split_axis=1, concat_axis=2, tiled=True),
        lax.all_to_all(marks, "clu", split_axis=1, concat_axis=2, tiled=True),
    )
    best = cluster_scores(arrived)
    returned = lax.all_to_all(best, "clu", split_axis=2, concat_axis=1, tiled=True)
    return returned.reshape(total)[slot]


def solution(mesh):
    in_specs = (P(("lang", "clu"), None), P(("lang", "clu"), None))
    out_specs = P(("lang", "clu"))
    return jax.shard_map(shards, mesh=mesh, in_specs=in_specs, out_specs=out_specs, check_vma=False)
```

profile of v0, /device:TPU:0, one launch (start us, length us, event | category | flops | bytes accessed | tf_op | source)
XLA Modules:
  0.0 87.9 jit_solution(13854131566071930487)
XLA Ops:
  0.0 0.7 copy-done
  0.7 3.2 %sort.17 = (s32[256]{0:T(256)}, s32[256]{0:T(256)S(1)}) sort(s32[256]{0:T(256)S(1)} %bitcast.15, s32[256]{0:T(256)S(1)} %iota.14), dimensions={0}, to_apply=%region_0.0 | sort | flops 2048 | bytes 4096 | tf_op jit(solution)/shard_map/jit(argsort)/sort | solution.py:20
  3.9 1.9 %gather_fusion.1 = s32[256]{0:T(256)S(1)} fusion(s32[256]{0:T(256)S(1)} %bitcast.16, s32[1024]{0:T(1024)S(1)} %pad_clamp_fusion.2), kind=kCustom, calls=%fused_computation.1 | custom fusion | bytes 3072 | tf_op jit(solution)/shard_map/gather | solution.py:21
  5.8 18.4 %while.37 = (s32[]{:T(128)}, u32[256]{0:T(256)S(1)}, u32[256]{0:T(256)S(1)}, s32[256]{0:T(256)S(1)}, s32[]{:T(128)}, /*index=5*/s32[]{:T(128)}, s32[]{}) while((s32[]{:T(128)}, u32[256]{0:T(256)S(1)}, u32[256]{0:T(256)S(1)}, s32[256]{0:T(256)S(1)}, s32[]{:T(128)}, /*index=5*/s32[]{:T(128)}, s32[]{}) %tuple.52), condition=%wide.region_2.3_spmd.clone, body=%wide.region_1.0_spmd.clone.sunk | while | flops 5636 | bytes 22117 | solution.py:22
  5.9 1.9 %gather_fusion = s32[256]{0:T(256)S(1)} fusion(s32[256]{0:T(256)S(1)} %get-tuple-element.217, u32[1024]{0:T(1024)S(1)} %pad_clamp_fusion.4), kind=kCustom, calls=%fused_computation.clone.clone.1 | custom fusion | bytes 3072 | tf_op jit(solution)/shard_map/jit(searchsorted)/jit(_searchsorted_scan_impl)/vmap(jit(_searchsorted_scan_impl))/while/body/eval_jaxpr/gather | solution.py:22
  7.9 1.9 %gather_fusion = s32[256]{0:T(256)S(1)} fusion(s32[256]{0:T(256)S(1)} %get-tuple-element.217, u32[1024]{0:T(1024)S(1)} %pad_clamp_fusion.4), kind=kCustom, calls=%fused_computation.clone.clone.1 | custom fusion | bytes 3072 | tf_op jit(solution)/shard_map/jit(searchsorted)/jit(_searchsorted_scan_impl)/vmap(jit(_searchsorted_scan_impl))/while/body/eval_jaxpr/gather | solution.py:22
  9.9 1.9 %gather_fusion = s32[256]{0:T(256)S(1)} fusion(s32[256]{0:T(256)S(1)} %get-tuple-element.217, u32[1024]{0:T(1024)S(1)} %pad_clamp_fusion.4), kind=kCustom, calls=%fused_computation.clone.clone.1 | custom fusion | bytes 3072 | tf_op jit(solution)/shard_map/jit(searchsorted)/jit(_searchsorted_scan_impl)/vmap(jit(_searchsorted_scan_impl))/while/body/eval_jaxpr/gather | solution.py:22
  12.0 1.9 %gather_fusion = s32[256]{0:T(256)S(1)} fusion(s32[256]{0:T(256)S(1)} %get-tuple-element.217, u32[1024]{0:T(1024)S(1)} %pad_clamp_fusion.4), kind=kCustom, calls=%fused_computation.clone.clone.1 | custom fusion | bytes 3072 | tf_op jit(solution)/shard_map/jit(searchsorted)/jit(_searchsorted_scan_impl)/vmap(jit(_searchsorted_scan_impl))/while/body/eval_jaxpr/gather | solution.py:22
  14.0 1.9 %gather_fusion = s32[256]{0:T(256)S(1)} fusion(s32[256]{0:T(256)S(1)} %get-tuple-element.217, u32[1024]{0:T(1024)S(1)} %pad_clamp_fusion.4), kind=kCustom, calls=%fused_computation.clone.clone.1 | custom fusion | bytes 3072 | tf_op jit(solution)/shard_map/jit(searchsorted)/jit(_searchsorted_scan_impl)/vmap(jit(_searchsorted_scan_impl))/while/body/eval_jaxpr/gather | solution.py:22
  16.1 1.9 %gather_fusion = s32[256]{0:T(256)S(1)} fusion(s32[256]{0:T(256)S(1)} %get-tuple-element.217, u32[1024]{0:T(1024)S(1)} %pad_clamp_fusion.4), kind=kCustom, calls=%fused_computation.clone.clone.1 | custom fusion | bytes 3072 | tf_op jit(solution)/shard_map/jit(searchsorted)/jit(_searchsorted_scan_impl)/vmap(jit(_searchsorted_scan_impl))/while/body/eval_jaxpr/gather | solution.py:22
  18.1 1.9 %gather_fusion = s32[256]{0:T(256)S(1)} fusion(s32[256]{0:T(256)S(1)} %get-tuple-element.217, u32[1024]{0:T(1024)S(1)} %pad_clamp_fusion.4), kind=kCustom, calls=%fused_computation.clone.clone.1 | custom fusion | bytes 3072 | tf_op jit(solution)/shard_map/jit(searchsorted)/jit(_searchsorted_scan_impl)/vmap(jit(_searchsorted_scan_impl))/while/body/eval_jaxpr/gather | solution.py:22
  20.1 1.9 %gather_fusion = s32[256]{0:T(256)S(1)} fusion(s32[256]{0:T(256)S(1)} %get-tuple-element.217, u32[1024]{0:T(1024)S(1)} %pad_clamp_fusion.4), kind=kCustom, calls=%fused_computation.clone.clone.1 | custom fusion | bytes 3072 | tf_op jit(solution)/shard_map/jit(searchsorted)/jit(_searchsorted_scan_impl)/vmap(jit(_searchsorted_scan_impl))/while/body/eval_jaxpr/gather | solution.py:22
  22.2 1.9 %gather_fusion = s32[256]{0:T(256)S(1)} fusion(s32[256]{0:T(256)S(1)} %get-tuple-element.217, u32[1024]{0:T(1024)S(1)} %pad_clamp_fusion.4), kind=kCustom, calls=%fused_computation.clone.clone.1 | custom fusion | bytes 3072 | tf_op jit(solution)/shard_map/jit(searchsorted)/jit(_searchsorted_scan_impl)/vmap(jit(_searchsorted_scan_impl))/while/body/eval_jaxpr/gather | solution.py:22
  24.2 1.4 %scatter_custom_fusion = s32[256]{0:T(256)S(1)} fusion(s32[256]{0:T(256)S(1)} %compare_select_fusion.1, s32[256]{0:T(256)S(1)} %convert_subtract_fusion, s32[]{:T(128)} %constant.83.clone.1), kind=kCustom, calls=%fused_computation.42 | custom fusion | bytes 1028 | tf_op jit(solution)/shard_map/scatter | solution.py:24
  25.6 2.2 %scatter_custom_fusion.1 = bf16[512]{0:T(512)(128)(2,1)S(1)} fusion(s32[256]{0:T(256)S(1)} %compare_select_fusion, bf16[256]{0:T(256)(128)(2,1)S(1)} %broadcast.47, bf16[]{:T(256)} %constant.85.clone.1), kind=kCustom, calls=%fused_computation.44 | custom fusion | bytes 1026 | tf_op jit(solution)/shard_map/scatter | solution.py:62
  27.9 0.6 copy.5
  28.5 7.4 %all-to-all-start = ((bf16[2,16,16]{2,0,1:T(2,128)(2,1)}), bf16[2,16,16]{2,0,1:T(2,128)(2,1)S(1)}, u32[]{:S(2)}, u32[]{:S(2)}) async-start(bf16[2,16,16]{2,0,1:T(2,128)(2,1)} %copy.5), calls=%async_computation | async-start | bytes 16384 | tf_op jit(solution)/shard_map/all_to_all | solution.py:67
  35.9 0.2 fusion.9
  36.1 2.0 %scatter_custom_fusion.2 = bf16[512,1024]{1,0:T(8,128)(2,1)S(1)} fusion(s32[256]{0:T(256)S(1)} %compare_select_fusion, bf16[256,1024]{1,0:T(8,128)(2,1)S(1)} %copy-done.1, f32[256]{0:T(256)S(1)} %add_rsqrt_fusion, bf16[]{:T(256)} %constant.85.clone.1), kind=kCustom, calls=%fused_computation.26 | custom fusion | flops 786432 | bytes 1573890 | tf_op jit(solution)/shard_map/scatter | solution.py:61
  38.1 1.1 %copy.7 = bf16[2,16,16,1024]{3,2,0,1:T(8,128)(2,1)} copy(bf16[2,16,16,1024]{3,2,1,0:T(8,128)(2,1)S(1)} %bitcast.19) | data formatting | bytes 2097152 | tf_op jit(solution)/shard_map/reshape | solution.py:63
  39.2 3.2 %all-to-all-done = bf16[2,16,16]{2,0,1:T(2,128)(2,1)S(1)} async-done(((bf16[2,16,16]{2,0,1:T(2,128)(2,1)}), bf16[2,16,16]{2,0,1:T(2,128)(2,1)S(1)}, u32[]{:S(2)}, u32[]{:S(2)}) %all-to-all-start) | async-done | bytes 1056 | tf_op jit(solution)/shard_map/all_to_all | solution.py:67
  42.3 3.7 %all-to-all-start.1 = ((bf16[2,16,16,1024]{3,2,0,1:T(8,128)(2,1)}), bf16[2,16,16,1024]{3,2,0,1:T(8,128)(2,1)S(1)}, u32[]{:S(2)}, u32[]{:S(2)}) async-start(bf16[2,16,16,1024]{3,2,0,1:T(8,128)(2,1)} %copy.7), calls=%async_computation.1 | async-start | bytes 2097152 | tf_op jit(solution)/shard_map/all_to_all | solution.py:66
  46.0 0.1 reshape.46
  46.1 22.7 %all-to-all-done.1 = bf16[2,16,16,1024]{3,2,0,1:T(8,128)(2,1)S(1)} async-done(((bf16[2,16,16,1024]{3,2,0,1:T(8,128)(2,1)}), bf16[2,16,16,1024]{3,2,0,1:T(8,128)(2,1)S(1)}, u32[]{:S(2)}, u32[]{:S(2)}) %all-to-all-start.1) | async-done | bytes 1048608 | tf_op jit(solution)/shard_map/all_to_all | solution.py:66
  68.8 0.1 copy.8
  68.9 0.9 %while.36 = (s32[]{:T(128)}, f32[2,256]{1,0:T(2,128)S(1)}, bf16[2,256]{1,0:T(2,128)(2,1)S(1)}, bf16[2,256,1024]{2,1,0:T(8,128)(2,1)S(1)}, s32[]{:T(128)}, /*index=5*/s32[]{:T(128)}) while((s32[]{:T(128)}, f32[2,256]{1,0:T(2,128)S(1)}, bf16[2,256]{1,0:T(2,128)(2,1)S(1)}, bf16[2,256,1024]{2,1,0:T(8,128)(2,1)S(1)}, s32[]{:T(128)}, ...), condition=%wide.region_9.10_spmd.clone, body=%wide.region_7.9_spmd.clone.sunk | while | flops 134480640 | bytes 530769 | solution.py:48
  69.0 0.4 fusion.26
  69.4 0.4 fusion.26
  69.8 0.8 copy.9
  70.6 6.7 %all-to-all-start.2 = ((f32[2,1,256]{0,1,2:T(1,128)}), f32[2,1,256]{0,1,2:T(1,128)S(1)}, u32[]{:S(2)}, u32[]{:S(2)}) async-start(f32[2,1,256]{0,1,2:T(1,128)} %bitcast.3), calls=%async_computation.2 | async-start | bytes 262144 | tf_op jit(solution)/shard_map/all_to_all | solution.py:70
  77.4 7.9 %all-to-all-done.2 = f32[2,1,256]{0,1,2:T(1,128)S(1)} async-done(((f32[2,1,256]{0,1,2:T(1,128)}), f32[2,1,256]{0,1,2:T(1,128)S(1)}, u32[]{:S(2)}, u32[]{:S(2)}) %all-to-all-start.2) | async-done | bytes 2080 | tf_op jit(solution)/shard_map/all_to_all | solution.py:70
  85.4 2.5 %gather_fusion.2 = f32[256]{0:T(256)} fusion(f32[512]{0:T(512)S(1)} %bitcast.18, s32[1024]{0:T(1024)S(1)} %pad_clamp_fusion.1), kind=kCustom, calls=%fused_computation.2 | custom fusion | bytes 3072 | tf_op jit(solution)/shard_map/gather | solution.py:71
  (69 shorter events, 0.7 us)
Async XLA Ops:
  0.0 0.7 copy-start
  5.8 30.1 %copy-start.1 = (bf16[256,1024]{1,0:T(8,128)(2,1)S(1)}, bf16[256,1024]{1,0:T(8,128)(2,1)}, u32[]{:S(2)}) copy-start(bf16[256,1024]{1,0:T(8,128)(2,1)} %param.6) | copy-start | bytes 1572868
  28.5 13.8 %all-to-all-start = ((bf16[2,16,16]{2,0,1:T(2,128)(2,1)}), bf16[2,16,16]{2,0,1:T(2,128)(2,1)S(1)}, u32[]{:S(2)}, u32[]{:S(2)}) async-start(bf16[2,16,16]{2,0,1:T(2,128)(2,1)} %copy.5), calls=%async_computation | async-start | bytes 16384 | tf_op jit(solution)/shard_map/all_to_all | solution.py:67
  42.3 26.5 %all-to-all-start.1 = ((bf16[2,16,16,1024]{3,2,0,1:T(8,128)(2,1)}), bf16[2,16,16,1024]{3,2,0,1:T(8,128)(2,1)S(1)}, u32[]{:S(2)}, u32[]{:S(2)}) async-start(bf16[2,16,16,1024]{3,2,0,1:T(8,128)(2,1)} %copy.7), calls=%async_computation.1 | async-start | bytes 2097152 | tf_op jit(solution)/shard_map/all_to_all | solution.py:66
  70.6 14.6 %all-to-all-start.2 = ((f32[2,1,256]{0,1,2:T(1,128)}), f32[2,1,256]{0,1,2:T(1,128)S(1)}, u32[]{:S(2)}, u32[]{:S(2)}) async-start(f32[2,1,256]{0,1,2:T(1,128)} %bitcast.3), calls=%async_computation.2 | async-start | bytes 262144 | tf_op jit(solution)/shard_map/all_to_all | solution.py:70
where the time goes:
time: 88.2 us; the launch traced here: 87.9 us
  waiting for transfers between devices  33.8 us (38%)
  local copies, waits for them, and re-layouts  29.1 us (33%)
  starting transfers between devices  17.8 us (20%)
  other arithmetic  5.78 us (7%)
    all_to_all x1, waiting for transfers between devices, shards(): lax.all_to_all(outgoing, 'clu', split_axis=1, concat_axis=2, tiled=True)  22.7 us
    gather x9, local copies, waits for them, and re-layouts, slot_index(): first = jnp.searchsorted(ranked, ranked, side='left')  17.5 us
    all_to_all x1, waiting for transfers between devices, shards(): lax.all_to_all(best, 'clu', split_axis=2, concat_axis=1, tiled=True)  7.89 us
    all_to_all x1, starting transfers between devices, shards(): lax.all_to_all(marks, 'clu', split_axis=1, concat_axis=2, tiled=True)  7.39 us
    all_to_all x1, starting transfers between devices, shards(): lax.all_to_all(best, 'clu', split_axis=2, concat_axis=1, tiled=True)  6.74 us
    all_to_all x1, starting transfers between devices, shards(): lax.all_to_all(outgoing, 'clu', split_axis=1, concat_axis=2, tiled=True)  3.65 us
    all_to_all x1, waiting for transfers between devices, shards(): lax.all_to_all(marks, 'clu', split_axis=1, concat_axis=2, tiled=True)  3.18 us
    sort x1, other arithmetic, slot_index(): order = jnp.argsort(cluster, stable=True)  3.16 us
  transfers between devices with their start and end apart: 3, of which 3 were waited for; matrix products, arithmetic and copies ran while one was open for 4% of the time, Pallas kernels for 0%

commit v1 on v0

--- a/solution.py
+++ b/solution.py
@@ -1,18 +1,172 @@
+import functools
+
 import jax
 import jax.numpy as jnp
 from jax import lax
+from jax.experimental import pallas as pl
+from jax.experimental.pallas import tpu as pltpu
 from jax.sharding import PartitionSpec as P
 
 CLU_DEV = 2
-
-
+LANES = 128
 EPS = 1e-06
+DEAD = 4.0
 
 
 def normalize(embeddings):
     values = embeddings.astype(jnp.float32)
     scale = lax.rsqrt(jnp.sum(values * values, axis=-1, keepdims=True) + EPS)
     return (values * scale).astype(jnp.bfloat16)
+
+
+def exchange_kernel(
+    groups, most, emb_ref, cluster_ref, out_ref,
+    unit, outgoing, arrived, best, returned,
+    load_sem, send_sem, recv_sem, back_send_sem, back_recv_sem,
+):
+    count, width = unit.shape
+    block = CLU_DEV * most
+    total = groups * block
+    me = lax.axis_index("clu")
+    chunks = 4
+    step = count // chunks
+
+    def load(c):
+        rows = pl.ds(c * step, step)
+        return pltpu.make_async_copy(emb_ref.at[rows], unit.at[rows], load_sem.at[c])
+
+    for c in range(chunks):
+        load(c).start()
+
+    barrier = pltpu.get_barrier_semaphore()
+    for k in range(1, groups):
+        pl.semaphore_signal(
+            barrier, inc=1, device_id={"clu": me ^ k}, device_id_type=pl.DeviceIdType.MESH
+        )
+
+    cluster_row = cluster_ref[...]
+    row_id = lax.broadcasted_iota(jnp.int32, (count, count), 0)
+    col_id = lax.broadcasted_iota(jnp.int32, (count, count), 1)
+    spread = jnp.broadcast_to(cluster_row, (count, count))
+    cluster_col = jnp.sum(jnp.where(row_id == col_id, spread, 0), axis=1, keepdims=True)
+    same = cluster_col == spread
+    rank_row = jnp.sum(jnp.where(same & (row_id < col_id), 1, 0), axis=0, keepdims=True)
+    slot_row = cluster_row * most + rank_row
+    slot_id = lax.broadcasted_iota(jnp.int32, (total, count), 0)
+    hit = slot_id == jnp.broadcast_to(slot_row, (total, count))
+    place = jnp.where(hit, 1.0, 0.0)
+    live = jnp.max(place, axis=1, keepdims=True)
+    place = place.astype(jnp.bfloat16)
+
+    for c in range(chunks):
+        load(c).wait()
+        rows = pl.ds(c * step, step)
+        unit[rows, :] = normalize(unit[rows, :])
+
+    outgoing[...] = jnp.dot(
+        place, unit[...], preferred_element_type=jnp.float32
+    ).astype(jnp.bfloat16)
+    lane = lax.broadcasted_iota(jnp.int32, (total, LANES), 1)
+    head = outgoing[:, 0:LANES].astype(jnp.float32)
+    outgoing[:, 0:LANES] = jnp.where(
+        (lane == 0) & (live < 0.5), DEAD, head
+    ).astype(jnp.bfloat16)
+
+    pl.semaphore_wait(barrier, groups - 1)
+
+    mine = pl.ds(pl.multiple_of(me * block, block), block)
+
+    def send(k):
+        peer = me ^ k
+        return pltpu.make_async_remote_copy(
+            src_ref=outgoing.at[pl.ds(pl.multiple_of(peer * block, block), block)],
+            dst_ref=arrived.at[mine],
+            send_sem=send_sem.at[k],
+            recv_sem=recv_sem.at[k],
+            device_id={"clu": peer},
+            device_id_type=pl.DeviceIdType.MESH,
+        )
+
+    for k in range(groups - 1, 0, -1):
+        send(k).start()
+    arrived[mine, :] = outgoing[mine, :]
+
+    rank_col = jnp.sum(
+        jnp.where(same & (col_id < row_id), 1, 0), axis=1, keepdims=True
+    )
+    owner_col = cluster_col // CLU_DEV
+    place_col = (cluster_col % CLU_DEV) * most + rank_col + (me * block) % LANES
+
+    for k in range(1, groups):
+        send(k).wait()
+
+    rows = arrived[...]
+    gram = lax.dot_general(
+        rows, rows, (((1,), (1,)), ((), ())), preferred_element_type=jnp.float32
+    )
+    dead = rows[:, 0:1].astype(jnp.float32) > 2.0
+    one = lax.broadcasted_iota(jnp.int32, (total, total), 0)
+    two = lax.broadcasted_iota(jnp.int32, (total, total), 1)
+    local = ((one ^ two) & most) == 0
+    keep = local & (one != two) & jnp.logical_not(dead)
+    best[0] = jnp.maximum(
+        jnp.max(jnp.where(keep, gram, -2.0), axis=0, keepdims=True), -1.0
+    )
+
+    def back(k):
+        peer = me ^ k
+        lanes = pl.ds(pl.multiple_of(peer * block // LANES * LANES, LANES), LANES)
+        return pltpu.make_async_remote_copy(
+            src_ref=best.at[:, :, lanes],
+            dst_ref=returned.at[pl.ds(me, 1)],
+            send_sem=back_send_sem.at[k],
+            recv_sem=back_recv_sem.at[k],
+            device_id={"clu": peer},
+            device_id_type=pl.DeviceIdType.MESH,
+        )
+
+    for k in range(groups - 1, 0, -1):
+        back(k).start()
+    returned[me] = best[0, :, pl.ds(pl.multiple_of(me * block // LANES * LANES, LANES), LANES)]
+    for k in range(1, groups):
+        back(k).wait()
+
+    picked = jnp.zeros((count, LANES), jnp.float32)
+    for owner in range(groups):
+        picked = jnp.where(owner_col == owner, returned[owner], picked)
+    lane = lax.broadcasted_iota(jnp.int32, (count, LANES), 1)
+    result = jnp.sum(jnp.where(lane == place_col, picked, 0.0), axis=1, keepdims=True)
+    out_ref[...] = jnp.sum(jnp.where(row_id == col_id, result, 0.0), axis=0, keepdims=True)
+
+
+def kernel_shards(embeddings, assignment):
+    groups = lax.axis_size("clu")
+    count, width = embeddings.shape
+    most = 2 * count // (CLU_DEV * groups)
+    total = CLU_DEV * groups * most
+    out = pl.pallas_call(
+        functools.partial(exchange_kernel, groups, most),
+        out_shape=jax.ShapeDtypeStruct((1, count), jnp.float32),
+        in_specs=[
+            pl.BlockSpec(memory_space=pl.ANY),
+            pl.BlockSpec(memory_space=pltpu.VMEM),
+        ],
+        out_specs=pl.BlockSpec(memory_space=pltpu.VMEM),
+        scratch_shapes=[
+            pltpu.VMEM((count, width), jnp.bfloat16),
+            pltpu.VMEM((total, width), jnp.bfloat16),
+            pltpu.VMEM((total, width), jnp.bfloat16),
+            pltpu.VMEM((1, 1, total), jnp.float32),
+            pltpu.VMEM((groups, 1, LANES), jnp.float32),
+            pltpu.SemaphoreType.DMA((4,)),
+            pltpu.SemaphoreType.DMA((groups,)),
+            pltpu.SemaphoreType.DMA((groups,)),
+            pltpu.SemaphoreType.DMA((groups,)),
+            pltpu.SemaphoreType.DMA((groups,)),
+        ],
+        compiler_params=pltpu.CompilerParams(collective_id=0, has_side_effects=True),
+    )(embeddings, assignment.reshape(1, count))
+    return out.reshape(count)
 
 
 def slot_index(cluster, groups, most):
@@ -49,7 +203,7 @@
     return best.reshape(items, 1, width)
 
 
-def shards(embeddings, assignment):
+def general_shards(embeddings, assignment):
     groups = lax.axis_size("clu")
     count = embeddings.shape[0]
     width = embeddings.shape[1]
@@ -71,6 +225,17 @@
     return returned.reshape(total)[slot]
 
 
+def shards(embeddings, assignment):
+    groups = lax.axis_size("clu")
+    count = embeddings.shape[0]
+    most = 2 * count // (CLU_DEV * groups)
+    block = CLU_DEV * most
+    power = groups & (groups - 1) == 0 and most & (most - 1) == 0
+    if power and block % 16 == 0 and LANES % block == 0 and (groups * block) % LANES == 0:
+        return kernel_shards(embeddings, assignment)
+    return general_shards(embeddings, assignment)
+
+
 def solution(mesh):
     in_specs = (P(("lang", "clu"), None), P(("lang", "clu"), None))
     out_specs = P(("lang", "clu"))

time: 88.2 us -> 38.4 us (0.44)
  Pallas kernels: 0 us -> 37 us
  waiting for transfers between devices: 33.8 us -> 0 us
  local copies, waits for them, and re-layouts: 29.1 us -> 1.22 us
  starting transfers between devices: 17.8 us -> 0 us
  other arithmetic: 5.78 us -> 0 us
    pallas_call x0 -> x1, Pallas kernels: none -> 37 us  [kernel_shards(): pl.pallas_call(functools.partial(exchange_kernel, groups, most), out_shap...]
    all_to_all x3 -> x0, waiting for transfers between devices: 33.8 us -> none  [the longest x1 22.7 us: shards(): lax.all_to_all(outgoing, 'clu', split_axis=1, concat_axis=2, tiled=True)]
    gather x11 -> x0, local copies, waits for them, and re-layouts: 22 us -> none  [the longest x9 17.5 us: slot_index(): first = jnp.searchsorted(ranked, ranked, side='left')]
    all_to_all x3 -> x0, starting transfers between devices: 17.8 us -> none  [the longest x1 7.39 us: shards(): lax.all_to_all(marks, 'clu', split_axis=1, concat_axis=2, tiled=True)]
    scatter x2 -> x0, local copies, waits for them, and re-layouts: 3.56 us -> none  [the longest x1 2.16 us: shards(): jnp.zeros((total,), jnp.bfloat16).at[slot]]
    sort x1 -> x0, other arithmetic: 3.16 us -> none  [slot_index(): order = jnp.argsort(cluster, stable=True)]
    scatter x1 -> x0, other arithmetic: 1.98 us -> none  [shards(): outgoing = jnp.zeros((total, width), jnp.bfloat16).at[slot].set(unit)]
    reshape x4 -> x0, local copies, waits for them, and re-layouts: 1.85 us -> none  [the longest x1 1.07 us: shards(): outgoing = outgoing.reshape(CLU_DEV, groups, most, width)]
  transfers between devices with their start and end apart: 3 -> 0, of which waited for: 3 -> 0; matrix products, arithmetic and copies ran while one was open for 4% -> 0% of each run, Pallas kernels for 0% -> 0%
where the time goes in v1:
time: 38.4 us; the launch traced here: 38.3 us
  Pallas kernels  37 us (96%)
  local copies, waits for them, and re-layouts  1.22 us (3%)
    pallas_call x1, Pallas kernels, kernel_shards(): pl.pallas_call(functools.partial(exchange_kernel, groups, most), out_shap...  37 us
    unnamed x3, local copies, waits for them, and re-layouts  1.22 us

profile of v1, /device:TPU:0, one launch (start us, length us, event | category | flops | bytes accessed | tf_op | source)
XLA Modules:
  0.0 38.3 jit_solution(2438430831591764610)
XLA Ops:
  0.0 37.0 %shard_map.28 = f32[1,256]{1,0:T(1,128)} custom-call(bf16[256,1024]{1,0:T(8,128)(2,1)} %emb_ref.1, s32[1,256]{1,0:T(1,128)} %bitcast.3), custom_call_target="tpu_custom_call" | custom-call | tf_op jit(solution)/shard_map/pallas_call | solution.py:147
  37.0 0.0 copy-start
  37.1 0.7 %copy-done = f32[1,256]{1,0:T(1,128)S(1)} copy-done((f32[1,256]{1,0:T(1,128)S(1)}, f32[1,256]{1,0:T(1,128)}, u32[]{:S(2)}) %copy-start) | copy-done | bytes 1048
  37.7 0.6 %copy.4 = f32[256]{0:T(256)} copy(f32[256]{0:T(256)S(1)} %bitcast.2) | data formatting | bytes 2048
Async XLA Ops:
  37.0 0.7 %copy-start = (f32[1,256]{1,0:T(1,128)S(1)}, f32[1,256]{1,0:T(1,128)}, u32[]{:S(2)}) copy-start(f32[1,256]{1,0:T(1,128)} %shard_map.28) | copy-start | bytes 3076

commit v2 on v1

--- a/solution.py
+++ b/solution.py
@@ -87,7 +87,7 @@
             device_id_type=pl.DeviceIdType.MESH,
         )
 
-    for k in range(groups - 1, 0, -1):
+    for k in range(1, groups):
         send(k).start()
     arrived[mine, :] = outgoing[mine, :]
 

time: 38.4 us -> 38 us (0.990)
  Pallas kernels: 37 us -> 36.6 us
    pallas_call x1, Pallas kernels: 37 us -> 36.6 us  [kernel_shards(): pl.pallas_call(functools.partial(exchange_kernel, groups, most), out_shap...]
where the time goes in v2:
time: 38 us; the launch traced here: 37.8 us
  Pallas kernels  36.6 us (96%)
  local copies, waits for them, and re-layouts  1.22 us (3%)
    pallas_call x1, Pallas kernels, kernel_shards(): pl.pallas_call(functools.partial(exchange_kernel, groups, most), out_shap...  36.6 us
    unnamed x3, local copies, waits for them, and re-layouts  1.22 us

profile of v2, /device:TPU:0, one launch (start us, length us, event | category | flops | bytes accessed | tf_op | source)
XLA Modules:
  0.0 37.8 jit_solution(12896345559785107226)
XLA Ops:
  0.0 36.6 %shard_map.28 = f32[1,256]{1,0:T(1,128)} custom-call(bf16[256,1024]{1,0:T(8,128)(2,1)} %emb_ref.1, s32[1,256]{1,0:T(1,128)} %bitcast.3), custom_call_target="tpu_custom_call" | custom-call | tf_op jit(solution)/shard_map/pallas_call | solution.py:147
  36.6 0.0 copy-start
  36.6 0.7 %copy-done = f32[1,256]{1,0:T(1,128)S(1)} copy-done((f32[1,256]{1,0:T(1,128)S(1)}, f32[1,256]{1,0:T(1,128)}, u32[]{:S(2)}) %copy-start) | copy-done | bytes 1048
  37.3 0.6 %copy.4 = f32[256]{0:T(256)} copy(f32[256]{0:T(256)S(1)} %bitcast.2) | data formatting | bytes 2048
Async XLA Ops:
  36.6 0.7 %copy-start = (f32[1,256]{1,0:T(1,128)S(1)}, f32[1,256]{1,0:T(1,128)}, u32[]{:S(2)}) copy-start(f32[1,256]{1,0:T(1,128)} %shard_map.28) | copy-start | bytes 3076

commit v3 on v2

--- a/solution.py
+++ b/solution.py
@@ -27,6 +27,7 @@
     count, width = unit.shape
     block = CLU_DEV * most
     total = groups * block
+    batch = LANES // block
     me = lax.axis_index("clu")
     chunks = 4
     step = count // chunks
@@ -43,6 +44,10 @@
         pl.semaphore_signal(
             barrier, inc=1, device_id={"clu": me ^ k}, device_id_type=pl.DeviceIdType.MESH
         )
+
+    def slot_of(cluster, rank):
+        peer = (cluster // CLU_DEV) ^ me
+        return peer * block + (cluster % CLU_DEV) * most + rank
 
     cluster_row = cluster_ref[...]
     row_id = lax.broadcasted_iota(jnp.int32, (count, count), 0)
@@ -51,92 +56,93 @@
     cluster_col = jnp.sum(jnp.where(row_id == col_id, spread, 0), axis=1, keepdims=True)
     same = cluster_col == spread
     rank_row = jnp.sum(jnp.where(same & (row_id < col_id), 1, 0), axis=0, keepdims=True)
-    slot_row = cluster_row * most + rank_row
-    slot_id = lax.broadcasted_iota(jnp.int32, (total, count), 0)
-    hit = slot_id == jnp.broadcast_to(slot_row, (total, count))
-    place = jnp.where(hit, 1.0, 0.0)
-    live = jnp.max(place, axis=1, keepdims=True)
-    place = place.astype(jnp.bfloat16)
+    slot_row = jnp.broadcast_to(slot_of(cluster_row, rank_row), (LANES, count))
 
     for c in range(chunks):
         load(c).wait()
         rows = pl.ds(c * step, step)
         unit[rows, :] = normalize(unit[rows, :])
 
-    outgoing[...] = jnp.dot(
-        place, unit[...], preferred_element_type=jnp.float32
-    ).astype(jnp.bfloat16)
-    lane = lax.broadcasted_iota(jnp.int32, (total, LANES), 1)
-    head = outgoing[:, 0:LANES].astype(jnp.float32)
-    outgoing[:, 0:LANES] = jnp.where(
-        (lane == 0) & (live < 0.5), DEAD, head
-    ).astype(jnp.bfloat16)
-
-    pl.semaphore_wait(barrier, groups - 1)
-
-    mine = pl.ds(pl.multiple_of(me * block, block), block)
-
     def send(k):
-        peer = me ^ k
+        rows = pl.ds(k * block, block)
         return pltpu.make_async_remote_copy(
-            src_ref=outgoing.at[pl.ds(pl.multiple_of(peer * block, block), block)],
-            dst_ref=arrived.at[mine],
+            src_ref=outgoing.at[rows],
+            dst_ref=arrived.at[rows],
             send_sem=send_sem.at[k],
             recv_sem=recv_sem.at[k],
-            device_id={"clu": peer},
+            device_id={"clu": me ^ k},
             device_id_type=pl.DeviceIdType.MESH,
         )
 
-    for k in range(1, groups):
-        send(k).start()
-    arrived[mine, :] = outgoing[mine, :]
+    first = lax.broadcasted_iota(jnp.int32, (count, LANES), 1) == 0
+    mark = jnp.where(first, DEAD, 0.0).astype(jnp.bfloat16)
+    blank = jnp.where(
+        lax.broadcasted_iota(jnp.int32, (LANES, LANES), 1) == 0, DEAD, 0.0
+    )
+    for g in range(groups // batch):
+        rows = pl.ds(g * LANES, LANES)
+        hit = lax.broadcasted_iota(jnp.int32, (LANES, count), 0) + g * LANES == slot_row
+        place = jnp.where(hit, 1.0, 0.0).astype(jnp.bfloat16)
+        packed = jnp.dot(place, unit[...], preferred_element_type=jnp.float32)
+        used = jnp.dot(place, mark, preferred_element_type=jnp.float32)
+        outgoing[rows, :] = packed.astype(jnp.bfloat16)
+        outgoing[rows, 0:LANES] = (packed[:, 0:LANES] + (blank - used)).astype(jnp.bfloat16)
+        if g == 0:
+            pl.semaphore_wait(barrier, groups - 1)
+        for k in range(max(1, g * batch), (g + 1) * batch):
+            send(k).start()
+    arrived[0:block, :] = outgoing[0:block, :]
 
     rank_col = jnp.sum(
         jnp.where(same & (col_id < row_id), 1, 0), axis=1, keepdims=True
     )
-    owner_col = cluster_col // CLU_DEV
-    place_col = (cluster_col % CLU_DEV) * most + rank_col + (me * block) % LANES
-
-    for k in range(1, groups):
-        send(k).wait()
-
-    rows = arrived[...]
-    gram = lax.dot_general(
-        rows, rows, (((1,), (1,)), ((), ())), preferred_element_type=jnp.float32
-    )
-    dead = rows[:, 0:1].astype(jnp.float32) > 2.0
-    one = lax.broadcasted_iota(jnp.int32, (total, total), 0)
-    two = lax.broadcasted_iota(jnp.int32, (total, total), 1)
-    local = ((one ^ two) & most) == 0
-    keep = local & (one != two) & jnp.logical_not(dead)
-    best[0] = jnp.maximum(
-        jnp.max(jnp.where(keep, gram, -2.0), axis=0, keepdims=True), -1.0
-    )
+    slot_col = slot_of(cluster_col, rank_col)
+    peer_col = slot_col // block
+    chosen = lax.broadcasted_iota(jnp.int32, (count, LANES), 1) == slot_col % LANES
+
+    def scores(one, two):
+        left, right = arrived[one[0] : one[1], :], arrived[two[0] : two[1], :]
+        gram = lax.dot_general(
+            left, right, (((1,), (1,)), ((), ())), preferred_element_type=jnp.float32
+        )
+        dead = left[:, 0:1].astype(jnp.float32) > 2.0
+        this = lax.broadcasted_iota(jnp.int32, gram.shape, 0) + one[0]
+        other = lax.broadcasted_iota(jnp.int32, gram.shape, 1) + two[0]
+        keep = (((this ^ other) & most) == 0) & (this != other) & jnp.logical_not(dead)
+        return jnp.max(jnp.where(keep, gram, -1.0), axis=0, keepdims=True)
+
+    for g in range(groups // batch):
+        low, high = g * LANES, (g + 1) * LANES
+        for k in range(max(1, g * batch), (g + 1) * batch):
+            send(k).wait_recv()
+        if g:
+            best[0, :, 0:low] = jnp.maximum(best[0, :, 0:low], scores((low, high), (0, low)))
+        best[0, :, low:high] = jnp.maximum(scores((0, high), (low, high)), -1.0)
 
     def back(k):
-        peer = me ^ k
-        lanes = pl.ds(pl.multiple_of(peer * block // LANES * LANES, LANES), LANES)
         return pltpu.make_async_remote_copy(
-            src_ref=best.at[:, :, lanes],
-            dst_ref=returned.at[pl.ds(me, 1)],
+            src_ref=best.at[:, :, pl.ds(k // batch * LANES, LANES)],
+            dst_ref=returned.at[pl.ds(k, 1)],
             send_sem=back_send_sem.at[k],
             recv_sem=back_recv_sem.at[k],
-            device_id={"clu": peer},
+            device_id={"clu": me ^ k},
             device_id_type=pl.DeviceIdType.MESH,
         )
 
     for k in range(groups - 1, 0, -1):
         back(k).start()
-    returned[me] = best[0, :, pl.ds(pl.multiple_of(me * block // LANES * LANES, LANES), LANES)]
+    returned[0] = best[0, :, 0:LANES]
+    for k in range(1, groups):
+        send(k).wait_send()
     for k in range(1, groups):
         back(k).wait()
 
     picked = jnp.zeros((count, LANES), jnp.float32)
-    for owner in range(groups):
-        picked = jnp.where(owner_col == owner, returned[owner], picked)
-    lane = lax.broadcasted_iota(jnp.int32, (count, LANES), 1)
-    result = jnp.sum(jnp.where(lane == place_col, picked, 0.0), axis=1, keepdims=True)
-    out_ref[...] = jnp.sum(jnp.where(row_id == col_id, result, 0.0), axis=0, keepdims=True)
+    for k in range(groups):
+        picked = jnp.where(peer_col == k, returned[k], picked)
+    result = jnp.sum(jnp.where(chosen, picked, 0.0), axis=1, keepdims=True)
+    result = jnp.sum(jnp.where(row_id == col_id, result, 0.0), axis=0, keepdims=True)
+    out_ref[...] = result.reshape(out_ref.shape)
 
 
 def kernel_shards(embeddings, assignment):
@@ -144,9 +150,9 @@
     count, width = embeddings.shape
     most = 2 * count // (CLU_DEV * groups)
     total = CLU_DEV * groups * most
-    out = pl.pallas_call(
+    return pl.pallas_call(
         functools.partial(exchange_kernel, groups, most),
-        out_shape=jax.ShapeDtypeStruct((1, count), jnp.float32),
+        out_shape=jax.ShapeDtypeStruct((count,), jnp.float32),
         in_specs=[
             pl.BlockSpec(memory_space=pl.ANY),
             pl.BlockSpec(memory_space=pltpu.VMEM),
@@ -166,7 +172,6 @@
         ],
         compiler_params=pltpu.CompilerParams(collective_id=0, has_side_effects=True),
     )(embeddings, assignment.reshape(1, count))
-    return out.reshape(count)
 
 
 def slot_index(cluster, groups, most):

time: 38 us -> 38.4 us (1.011)
  Pallas kernels: 36.6 us -> 37 us
    pallas_call x1, Pallas kernels: 36.6 us -> 37 us  [kernel_shards(): pl.pallas_call(functools.partial(exchange_kernel, groups, most), out_shap...]
    unnamed x3 -> x1, local copies, waits for them, and re-layouts: 1.22 us -> 1.24 us
where the time goes in v3:
time: 38.4 us; the launch traced here: 38.3 us
  Pallas kernels  37 us (96%)
  local copies, waits for them, and re-layouts  1.24 us (3%)
    pallas_call x1, Pallas kernels, kernel_shards(): pl.pallas_call(functools.partial(exchange_kernel, groups, most), out_shap...  37 us
    unnamed x1, local copies, waits for them, and re-layouts  1.24 us

profile of v3, /device:TPU:0, one launch (start us, length us, event | category | flops | bytes accessed | tf_op | source)
XLA Modules:
  0.0 38.3 jit_solution(15929564325679396125)
XLA Ops:
  0.0 37.0 %shard_map.28 = f32[256]{0:T(256)} custom-call(bf16[256,1024]{1,0:T(8,128)(2,1)} %emb_ref.1, s32[1,256]{1,0:T(1,128)} %bitcast.1), custom_call_target="tpu_custom_call" | custom-call | tf_op jit(solution)/shard_map/pallas_call | solution.py:153
  37.0 1.2 %copy.4 = f32[256]{0:T(256)} copy(f32[256]{0:T(256)} %shard_map.28) | data formatting | bytes 2048

commit v4 on v3

--- a/solution.py
+++ b/solution.py
@@ -22,7 +22,7 @@
 def exchange_kernel(
     groups, most, emb_ref, cluster_ref, out_ref,
     unit, outgoing, arrived, best, returned,
-    load_sem, send_sem, recv_sem, back_send_sem, back_recv_sem,
+    load_sem, send_sem, recv_sem, back_send_sem, back_recv_sem, ready,
 ):
     count, width = unit.shape
     block = CLU_DEV * most
@@ -40,10 +40,23 @@
         load(c).start()
 
     barrier = pltpu.get_barrier_semaphore()
-    for k in range(1, groups):
+    bits = groups.bit_length() - 1
+    for b in range(bits):
         pl.semaphore_signal(
-            barrier, inc=1, device_id={"clu": me ^ k}, device_id_type=pl.DeviceIdType.MESH
-        )
+            barrier, inc=1, device_id={"clu": me ^ (1 << b)},
+            device_id_type=pl.DeviceIdType.MESH,
+        )
+
+    def tell(stage):
+        for b in range(bits):
+            pl.semaphore_signal(
+                ready.at[stage, b], inc=1, device_id={"clu": me ^ (1 << b)},
+                device_id_type=pl.DeviceIdType.MESH,
+            )
+
+    def hear(stage):
+        for b in range(bits):
+            pl.semaphore_wait(ready.at[stage, b], 1)
 
     def slot_of(cluster, rank):
         peer = (cluster // CLU_DEV) ^ me
@@ -64,7 +77,7 @@
         unit[rows, :] = normalize(unit[rows, :])
 
     def send(k):
-        rows = pl.ds(k * block, block)
+        rows = pl.ds(pl.multiple_of(k * block, block), block)
         return pltpu.make_async_remote_copy(
             src_ref=outgoing.at[rows],
             dst_ref=arrived.at[rows],
@@ -79,7 +92,9 @@
     blank = jnp.where(
         lax.broadcasted_iota(jnp.int32, (LANES, LANES), 1) == 0, DEAD, 0.0
     )
-    for g in range(groups // batch):
+    pl.semaphore_wait(barrier, bits)
+    tell(0)
+    for g in reversed(range(groups // batch)):
         rows = pl.ds(g * LANES, LANES)
         hit = lax.broadcasted_iota(jnp.int32, (LANES, count), 0) + g * LANES == slot_row
         place = jnp.where(hit, 1.0, 0.0).astype(jnp.bfloat16)
@@ -87,10 +102,14 @@
         used = jnp.dot(place, mark, preferred_element_type=jnp.float32)
         outgoing[rows, :] = packed.astype(jnp.bfloat16)
         outgoing[rows, 0:LANES] = (packed[:, 0:LANES] + (blank - used)).astype(jnp.bfloat16)
-        if g == 0:
-            pl.semaphore_wait(barrier, groups - 1)
-        for k in range(max(1, g * batch), (g + 1) * batch):
-            send(k).start()
+    for n in range(1, bits + 1):
+        if n > 1:
+            hear(n - 2)
+            if n < bits:
+                tell(n - 1)
+        for k in reversed(range(1, groups)):
+            if k.bit_count() == n:
+                send(k).start()
     arrived[0:block, :] = outgoing[0:block, :]
 
     rank_col = jnp.sum(
@@ -134,12 +153,12 @@
     returned[0] = best[0, :, 0:LANES]
     for k in range(1, groups):
         send(k).wait_send()
+    picked = jnp.broadcast_to(returned[0], (count, LANES))
     for k in range(1, groups):
-        back(k).wait()
-
-    picked = jnp.zeros((count, LANES), jnp.float32)
-    for k in range(groups):
+        back(k).wait_recv()
         picked = jnp.where(peer_col == k, returned[k], picked)
+    for k in range(1, groups):
+        back(k).wait_send()
     result = jnp.sum(jnp.where(chosen, picked, 0.0), axis=1, keepdims=True)
     result = jnp.sum(jnp.where(row_id == col_id, result, 0.0), axis=0, keepdims=True)
     out_ref[...] = result.reshape(out_ref.shape)
@@ -169,6 +188,7 @@
             pltpu.SemaphoreType.DMA((groups,)),
             pltpu.SemaphoreType.DMA((groups,)),
             pltpu.SemaphoreType.DMA((groups,)),
+            pltpu.SemaphoreType.REGULAR((groups.bit_length(), groups.bit_length())),
         ],
         compiler_params=pltpu.CompilerParams(collective_id=0, has_side_effects=True),
     )(embeddings, assignment.reshape(1, count))

time: 38.4 us -> 37.1 us (0.966)
  Pallas kernels: 37 us -> 35.7 us
    pallas_call x1, Pallas kernels: 37 us -> 35.7 us  [kernel_shards(): pl.pallas_call(functools.partial(exchange_kernel, groups, most), out_shap...]
where the time goes in v4:
time: 37.1 us; the launch traced here: 36.9 us
  Pallas kernels  35.7 us (96%)
  local copies, waits for them, and re-layouts  1.24 us (3%)
    pallas_call x1, Pallas kernels, kernel_shards(): pl.pallas_call(functools.partial(exchange_kernel, groups, most), out_shap...  35.7 us
    unnamed x1, local copies, waits for them, and re-layouts  1.24 us

profile of v4, /device:TPU:0, one launch (start us, length us, event | category | flops | bytes accessed | tf_op | source)
XLA Modules:
  0.0 36.9 jit_solution(14601248973396394330)
XLA Ops:
  0.0 35.7 %shard_map.28 = f32[256]{0:T(256)} custom-call(bf16[256,1024]{1,0:T(8,128)(2,1)} %emb_ref.1, s32[1,256]{1,0:T(1,128)} %bitcast.1), custom_call_target="tpu_custom_call" | custom-call | tf_op jit(solution)/shard_map/pallas_call | solution.py:172
  35.7 1.2 %copy.4 = f32[256]{0:T(256)} copy(f32[256]{0:T(256)} %shard_map.28) | data formatting | bytes 2048

commit v5 on v4

--- a/solution.py
+++ b/solution.py
@@ -94,7 +94,9 @@
     )
     pl.semaphore_wait(barrier, bits)
     tell(0)
-    for g in reversed(range(groups // batch)):
+    last = groups // batch - 1
+    order = sorted(range(groups // batch), key=lambda g: (g == last, -g))
+    for g in order:
         rows = pl.ds(g * LANES, LANES)
         hit = lax.broadcasted_iota(jnp.int32, (LANES, count), 0) + g * LANES == slot_row
         place = jnp.where(hit, 1.0, 0.0).astype(jnp.bfloat16)
@@ -102,15 +104,19 @@
         used = jnp.dot(place, mark, preferred_element_type=jnp.float32)
         outgoing[rows, :] = packed.astype(jnp.bfloat16)
         outgoing[rows, 0:LANES] = (packed[:, 0:LANES] + (blank - used)).astype(jnp.bfloat16)
+        for k in range(max(1, g * batch), (g + 1) * batch):
+            if k.bit_count() == 1:
+                send(k).start()
     for n in range(1, bits + 1):
         if n > 1:
             hear(n - 2)
             if n < bits:
                 tell(n - 1)
         for k in reversed(range(1, groups)):
-            if k.bit_count() == n:
+            if k.bit_count() == n and n > 1:
                 send(k).start()
     arrived[0:block, :] = outgoing[0:block, :]
+    best[0] = jnp.full((1, total), -1.0, jnp.float32)
 
     rank_col = jnp.sum(
         jnp.where(same & (col_id < row_id), 1, 0), axis=1, keepdims=True
@@ -134,9 +140,13 @@
         low, high = g * LANES, (g + 1) * LANES
         for k in range(max(1, g * batch), (g + 1) * batch):
             send(k).wait_recv()
+        best[0, :, 0:high] = jnp.maximum(
+            best[0, :, 0:high], scores((low, high), (0, high))
+        )
         if g:
-            best[0, :, 0:low] = jnp.maximum(best[0, :, 0:low], scores((low, high), (0, low)))
-        best[0, :, low:high] = jnp.maximum(scores((0, high), (low, high)), -1.0)
+            best[0, :, low:high] = jnp.maximum(
+                best[0, :, low:high], scores((0, low), (low, high))
+            )
 
     def back(k):
         return pltpu.make_async_remote_copy(

time: 37.1 us -> 36.8 us (level)
  no operation moved by 1% of the time
where the time goes in v5:
time: 36.8 us; the launch traced here: 36.6 us
  Pallas kernels  35.4 us (96%)
  local copies, waits for them, and re-layouts  1.24 us (3%)
    pallas_call x1, Pallas kernels, kernel_shards(): pl.pallas_call(functools.partial(exchange_kernel, groups, most), out_shap...  35.4 us
    unnamed x1, local copies, waits for them, and re-layouts  1.24 us

profile of v5, /device:TPU:0, one launch (start us, length us, event | category | flops | bytes accessed | tf_op | source)
XLA Modules:
  0.0 36.6 jit_solution(4162963329317231333)
XLA Ops:
  0.0 35.4 %shard_map.28 = f32[256]{0:T(256)} custom-call(bf16[256,1024]{1,0:T(8,128)(2,1)} %emb_ref.1, s32[1,256]{1,0:T(1,128)} %bitcast.1), custom_call_target="tpu_custom_call" | custom-call | tf_op jit(solution)/shard_map/pallas_call | solution.py:182
  35.4 1.2 %copy.4 = f32[256]{0:T(256)} copy(f32[256]{0:T(256)} %shard_map.28) | data formatting | bytes 2048
